TPU v7x, 32 devices: a whole 2x2x4 slice. The times are simulated.
32 devices in a mesh: row: 2 (over y), phi: 16 (over z, x, core).
Axes of the slice: x: 2, y: 2, z: 4, core: 2. Of those that a mesh axis runs over, the one named last changes fastest.
Arguments:
- density: float32 [32, 2048, 512], P('row', 'phi'), may hold values from 0.3 to 3
- velocity: float32 [3, 32, 2048, 512], P(None, 'row', 'phi'), may hold values from -3 to 3
- magnetic: float32 [3, 32, 2048, 512], P(None, 'row', 'phi'), may hold values from -6 to 6
Outputs:
- density_next: float32 [32, 2048, 512], P('row', 'phi')
- magnetic_next: float32 [3, 32, 2048, 512], P(None, 'row', 'phi')
All inputs are finite; a program needn't handle non-finite values.
Results may differ from a plain program's by a relative error of at most 0.0003.
Values sent between devices are 32-bit elements; how exact they have to be, the bound alone decides.
A program may use at most 256 MiB of HBM per device.

v0:
```python
from functools import partial
import jax
import jax.numpy as jnp
from jax import lax
from jax.sharding import PartitionSpec as P

NP = 2048
NPOL = 128
COURANT_RAD = 0.3
COURANT_POL = 0.25
COURANT_AZI = 0.35
SOUND_SPEED = 1.0


def extended(value, sides, width, wrap):
    for axis, dim in sides:
        devices, length = (lax.axis_size(axis), value.shape[dim])
        up = [(i, (i + 1) % devices) for i in range(devices if wrap else devices - 1)]
        down = [(j, i) for i, j in up]
        last = lax.slice_in_dim(value, length - width, length, axis=dim)
        leading = lax.slice_in_dim(value, 0, width, axis=dim)
        before = lax.ppermute(last, axis, up)
        after = lax.ppermute(leading, axis, down)
        value = jnp.concatenate([before, value, after], axis=dim)
    return value


def shift_theta(values, offset):
    if offset == 0:
        return values
    if offset > 0:
        border = jnp.repeat(values[..., -1:], offset, axis=-1)
        return jnp.concatenate([values[..., offset:], border], axis=-1)
    border = jnp.repeat(values[..., :1], -offset, axis=-1)
    return jnp.concatenate([border, values[..., :offset]], axis=-1)


def interface_value(outer_left, inner_left, inner_right, outer_right):
    guess = 7.0 / 12.0 * (inner_left + inner_right) - 1.0 / 12.0 * (outer_left + outer_right)
    return jnp.clip(
        guess, jnp.minimum(inner_left, inner_right), jnp.maximum(inner_left, inner_right)
    )


def edge_values(nearby):
    centre = nearby(0)
    left_face = interface_value(nearby(-2), nearby(-1), centre, nearby(1))
    right_face = interface_value(nearby(-1), centre, nearby(1), nearby(2))
    to_left = left_face - centre
    to_right = right_face - centre
    left_limited = jnp.clip(to_left, -2.0 * jnp.abs(to_right), 2.0 * jnp.abs(to_right))
    right_limited = jnp.clip(to_right, -2.0 * jnp.abs(to_left), 2.0 * jnp.abs(to_left))
    return (centre + left_limited, centre + right_limited)


def hll_flux(dens_left, dens_right, speed_left, speed_right):
    slowest = jnp.minimum(jnp.minimum(speed_left, speed_right) - SOUND_SPEED, 0.0)
    fastest = jnp.maximum(jnp.maximum(speed_left, speed_right) + SOUND_SPEED, 0.0)
    upwind = fastest * dens_left * speed_left - slowest * dens_right * speed_right
    return (upwind + slowest * fastest * (dens_right - dens_left)) / (fastest - slowest)


def axis_divergence(dens, speed, axis, count, ghost):

    def picker(field):

        def nearby(offset):
            return lax.slice_in_dim(
                field, ghost - 1 + offset, ghost + 1 + offset + count, axis=axis
            )

        return nearby

    def window(values, start, stop):
        return lax.slice_in_dim(values, start, stop, axis=axis)

    dens_left, dens_right = edge_values(picker(dens))
    speed_left, speed_right = edge_values(picker(speed))
    flux = hll_flux(
        window(dens_right, 0, count + 1),
        window(dens_left, 1, count + 2),
        window(speed_right, 0, count + 1),
        window(speed_left, 1, count + 2),
    )
    return window(flux, 1, count + 1) - window(flux, 0, count)


def theta_divergence(dens, speed):
    dens_left, dens_right = edge_values(partial(shift_theta, dens))
    speed_left, speed_right = edge_values(partial(shift_theta, speed))
    flux = hll_flux(
        shift_theta(dens_right, -1), dens_left, shift_theta(speed_right, -1), speed_left
    )
    position = lax.broadcasted_iota(jnp.int32, flux.shape, flux.ndim - 1)
    flux = jnp.where(position == 0, jnp.zeros_like(flux), flux)
    upper_flux = jnp.concatenate([flux[..., 1:], jnp.zeros_like(flux[..., :1])], axis=-1)
    return upper_flux - flux


def advance(primitive, magnetic, ghost, face_ghost, radial, azimuth):
    dens = primitive[0]
    radial_speed = primitive[1]
    polar_speed = primitive[2]
    azimuth_speed = primitive[3]

    def inner(values, width):
        return values[width : width + radial, width : width + azimuth]

    def box(values, width):
        return values[width - 1 : width + radial + 1, width - 1 : width + azimuth + 1]

    rad_term = axis_divergence(
        dens[:, ghost : ghost + azimuth], radial_speed[:, ghost : ghost + azimuth], 0, radial, ghost
    )
    azi_term = axis_divergence(
        dens[ghost : ghost + radial], azimuth_speed[ghost : ghost + radial], 1, azimuth, ghost
    )
    dens_inner = inner(dens, ghost)
    pol_term = theta_divergence(dens_inner, inner(polar_speed, ghost))
    density_next = (
        dens_inner - COURANT_RAD * rad_term - COURANT_POL * pol_term - COURANT_AZI * azi_term
    )
    radial_span = magnetic[0][
        face_ghost - 1 : face_ghost + radial + 2, face_ghost - 1 : face_ghost + azimuth + 1
    ]
    radial_cell = 0.5 * (radial_span[:-1] + radial_span[1:])
    azimuth_span = magnetic[2][
        face_ghost - 1 : face_ghost + radial + 1, face_ghost - 1 : face_ghost + azimuth + 2
    ]
    azimuth_cell = 0.5 * (azimuth_span[:, :-1] + azimuth_span[:, 1:])
    polar_box = box(magnetic[1], face_ghost)
    polar_cell = 0.5 * (polar_box + shift_theta(polar_box, 1))
    speed_r = box(radial_speed, ghost)
    speed_t = box(polar_speed, ghost)
    speed_p = box(azimuth_speed, ghost)
    radial_emf = -(speed_t * azimuth_cell - speed_p * polar_cell)
    polar_emf = -(speed_p * radial_cell - speed_r * azimuth_cell)
    azimuth_emf = -(speed_r * polar_cell - speed_t * radial_cell)
    radial_edge = 0.5 * (radial_emf[1 : radial + 1, :-1] + radial_emf[1 : radial + 1, 1:])
    radial_below = 0.5 * (shift_theta(radial_edge, -1) + radial_edge)
    radial_above = 0.5 * (radial_edge + shift_theta(radial_edge, 1))
    azimuth_edge = 0.5 * (azimuth_emf[:-1, 1 : azimuth + 1] + azimuth_emf[1:, 1 : azimuth + 1])
    azimuth_below = 0.5 * (shift_theta(azimuth_edge, -1) + azimuth_edge)
    azimuth_above = 0.5 * (azimuth_edge + shift_theta(azimuth_edge, 1))
    polar_edge = 0.25 * (
        polar_emf[:-1, :-1] + polar_emf[1:, :-1] + polar_emf[:-1, 1:] + polar_emf[1:, 1:]
    )
    radial_next = (
        inner(magnetic[0], face_ghost)
        - COURANT_POL * (azimuth_above[:radial] - azimuth_below[:radial])
        + COURANT_AZI * (polar_edge[:radial, 1:] - polar_edge[:radial, :-1])
    )
    polar_next = (
        inner(magnetic[1], face_ghost)
        - COURANT_AZI * (radial_below[:, 1:] - radial_below[:, :-1])
        + COURANT_RAD * (azimuth_below[1:] - azimuth_below[:-1])
    )
    azimuth_next = (
        inner(magnetic[2], face_ghost)
        - COURANT_RAD * (polar_edge[1:, :azimuth] - polar_edge[:-1, :azimuth])
        + COURANT_POL * (radial_above[:, :azimuth] - radial_below[:, :azimuth])
    )
    return (density_next, jnp.stack([radial_next, polar_next, azimuth_next]))


def radial_fix(padded, width):
    first_row = lax.axis_index("row") == 0
    last_row = lax.axis_index("row") == lax.axis_size("row") - 1
    inner_low = jnp.broadcast_to(padded[:, width : width + 1], padded[:, :width].shape)
    inner_high = jnp.broadcast_to(padded[:, -width - 1 : -width], padded[:, -width:].shape)
    low_side = jnp.where(first_row, inner_low, padded[:, :width])
    high_side = jnp.where(last_row, inner_high, padded[:, -width:])
    return jnp.concatenate([low_side, padded[:, width:-width], high_side], axis=1)


def ghost_state(values):
    padded = radial_fix(extended(values, (("row", 1),), 3, False), 3)
    result = extended(padded, (("phi", 2),), 3, True)
    return result


def per_device(density, velocity, magnetic):
    radial, azimuth, theta_count = density.shape
    half_polar = NPOL // 2
    primitive = jnp.concatenate([density[None], velocity], axis=0)
    polar_rows = jnp.concatenate(
        [primitive[..., :half_polar], primitive[..., theta_count - half_polar :]], axis=-1
    )
    polar_rows = jnp.swapaxes(polar_rows, 2, 3)
    column = lax.broadcasted_iota(jnp.int32, (NP, NP), 1)
    sample = lax.broadcasted_iota(jnp.int32, (NP, NP), 0)
    mode_index = jnp.where(column <= NP // 2, column, column - NP // 2)
    phase_angle = (sample * mode_index % NP).astype(jnp.float32) * (2.0 * jnp.pi / NP)
    fourier_basis = jnp.where(column <= NP // 2, jnp.cos(phase_angle), jnp.sin(phase_angle))
    mode_row = mode_index[0]
    column_row = column[0]
    weights = jnp.where((mode_row == 0) | (column_row == NP // 2), 1.0 / NP, 2.0 / NP).astype(
        jnp.float32
    )
    mode_sine = jnp.sin(jnp.pi * mode_row.astype(jnp.float32) / NP)
    edge_sine = jnp.sin(jnp.pi * (half_polar + 0.5) / theta_count)
    lines = lax.all_to_all(polar_rows, "phi", split_axis=2, concat_axis=3, tiled=True)
    local_rows = lines.shape[2]
    global_row = lax.axis_index("phi") * local_rows + jnp.arange(local_rows, dtype=jnp.int32)
    theta_row = jnp.where(global_row < half_polar, global_row, theta_count - NPOL + global_row)
    row_sine = jnp.sin(jnp.pi * (theta_row.astype(jnp.float32) + 0.5) / theta_count)
    row_square = (row_sine * row_sine)[:, None]
    mode_square = (edge_sine * mode_sine)[None, :]
    damping = row_square / jnp.maximum(row_square, mode_square * mode_square)
    spectrum = jnp.dot(
        lines.reshape(-1, NP),
        fourier_basis,
        precision=lax.Precision.HIGHEST,
        preferred_element_type=jnp.float32,
    ).reshape(lines.shape)
    spectrum = spectrum * (damping * weights[None, :])
    smoothed = lax.dot_general(
        spectrum.reshape(-1, NP),
        fourier_basis,
        (((1,), (1,)), ((), ())),
        precision=lax.Precision.HIGHEST,
        preferred_element_type=jnp.float32,
    ).reshape(lines.shape)
    returned = lax.all_to_all(smoothed, "phi", split_axis=3, concat_axis=2, tiled=True)
    returned = jnp.swapaxes(returned, 2, 3)
    primitive = jnp.concatenate(
        [
            returned[..., :half_polar],
            primitive[..., half_polar : theta_count - half_polar],
            returned[..., half_polar:],
        ],
        axis=-1,
    )
    state = ghost_state(jnp.concatenate([primitive, magnetic], axis=0))
    primitive_padded = state[:4]
    magnetic_padded = state[4:]
    face_ghost = 3
    return advance(primitive_padded, magnetic_padded, 3, face_ghost, radial, azimuth)


def solution(mesh):
    placed = (P("row", "phi", None), P(None, "row", "phi", None), P(None, "row", "phi", None))
    return jax.shard_map(
        per_device,
        mesh=mesh,
        in_specs=placed,
        out_specs=(P("row", "phi", None), P(None, "row", "phi", None)),
        check_vma=False,
    )
```

profile of v0, /device:TPU:13, one launch (start us, length us, event | category | flops | bytes accessed | tf_op | source)
XLA Modules:
  0.0 1016.8 jit_solution(8713738832390552506)
XLA Ops:
  11.4 6.5 all-to-all-start
  20.5 67.5 %fusion.152 = f32[2048,2048,1,1]{1,0,3,2:T(8,128)} fusion(s32[2048]{0:T(1024)S(1)} %iota_add_fusion, pred[2048]{0:T(1024)(128)(4,1)S(1)} %iota_compare_fusion.2), kind=kLoop, calls=%fused_computation.10.clone.1 | loop fusion | flops 67108864 | bytes 16787456 | tf_op jit(solution)/shard_map/dot_general | solution.py:210
  88.0 20.2 %all-to-all-done = f32[4,16,128,128]{3,1,0,2:T(8,128)} async-done(((f32[4,16,128,128]{3,1,0,2:T(8,128)}), f32[4,16,128,128]{3,1,0,2:T(8,128)}, u32[]{:S(2)}, u32[]{:S(2)}) %all-to-all-start) | async-done | bytes 4194336 | tf_op jit(solution)/shard_map/all_to_all | solution.py:202
  108.2 34.1 %fusion.5 = f32[4,16,8,2048]{3,2,1,0:T(8,128)S(1)} fusion(f32[4,16,128,128]{3,1,0,2:T(8,128)} %all-to-all-done, f32[2048,2048,1,1]{1,0,3,2:T(8,128)} %fusion.152), kind=kOutput, calls=%fused_computation.9 | convolution fusion | flops 25769803776 | bytes 25165824 | tf_op jit(solution)/shard_map/dot_general | solution.py:210
  142.6 94.4 %fusion.3 = f32[4,16,8,2048]{3,2,1,0:T(8,128)} fusion(pred[2048]{0:T(1024)(128)(4,1)S(1)} %iota_compare_fusion.2, s32[2048]{0:T(1024)S(1)} %iota_add_fusion, f32[4,16,8,2048]{3,2,1,0:T(8,128)S(1)} %fusion.150), kind=kOutput, calls=%fused_computation.7 | convolution fusion | flops 25836912640 | bytes 8398848 | tf_op jit(solution)/shard_map/dot_general | solution.py:217
  237.0 26.4 %copy.108 = f32[4,16,8,2048]{1,2,0,3:T(8,128)} copy(f32[4,16,8,2048]{3,2,1,0:T(8,128)} %fusion.3) | data formatting | bytes 8388608 | tf_op jit(solution)/shard_map/dot_general | solution.py:217
  263.4 22.0 %reshape.119 = f32[16,1,65536]{2,1,0:T(1,128)} reshape(f32[2048,4,8,16]{3,2,1,0:T(8,128)} %bitcast.95) | data formatting | bytes 8388608
  285.4 7.0 all-to-all-start.1
  292.4 11.6 %pad_maximum_fusion.1 = f32[4,16,128,384]{3,2,0,1:T(8,128)} fusion(f32[1,16,128,512]{3,2,0,1:T(8,128)} %bitcast.114, f32[3,16,128,512]{3,2,1,0:T(8,128)} %param.4), kind=kLoop, calls=%fused_computation.13 | loop fusion | flops 3145728 | bytes 29360128 | tf_op jit(solution)/shard_map/concatenate | solution.py:185
  304.0 78.6 %all-to-all-done.1 = f32[16,1,65536]{2,1,0:T(1,128)} async-done(((f32[16,1,65536]{2,1,0:T(1,128)}), f32[16,1,65536]{2,1,0:T(1,128)}, u32[]{:S(2)}, u32[]{:S(2)}) %all-to-all-start.1) | async-done | bytes 4194336 | tf_op jit(solution)/shard_map/all_to_all | solution.py:224
  383.1 13.7 %reduce.8 = f32[16,65536]{1,0:T(8,128)} reduce(f32[16,1,65536]{2,1,0:T(1,128)} %all-to-all-done.1, f32[]{:T(128)} %broadcast.356), dimensions={1}, to_apply=%all_to_all.27.reduce_sub_computation | reduce | bytes 8388612 | tf_op jit(solution)/shard_map/all_to_all | solution.py:224
  396.8 25.8 %reshape.120 = f32[2048,4,8,16]{3,2,1,0:T(8,128)} reshape(f32[16,65536]{1,0:T(8,128)} %reduce.8) | data formatting | bytes 8388608
  422.6 21.1 %copy.110 = f32[4,16,16,8,128]{4,3,2,1,0:T(8,128)} copy(f32[4,16,16,8,128]{1,3,0,4,2:T(8,128)} %bitcast.96) | data formatting | bytes 8388608 | tf_op jit(solution)/shard_map/all_to_all | solution.py:224
  454.4 6.3 pad_maximum_fusion.6
  477.4 106.1 %collective-permute-done.1 = f32[7,3,128,512]{3,2,1,0:T(8,128)} collective-permute-done((f32[7,3,128,512]{3,2,1,0:T(8,128)}, f32[7,3,128,512]{3,2,1,0:T(8,128)}, u32[]{:S(2)}, u32[]{:S(2)}) %collective-permute-start.1) | collective-permute-done | bytes 5505056 | tf_op jit(solution)/shard_map/ppermute | solution.py:23
  593.1 7.3 copy_select_fusion.1
  611.4 21.4 %collective-permute-done.3 = f32[7,22,3,512]{3,1,2,0:T(8,128)S(1)} collective-permute-done((f32[7,22,3,512]{3,1,2,0:T(8,128)S(1)}, f32[7,22,3,512]{3,1,2,0:T(8,128)S(1)}, u32[]{:S(2)}, u32[]{:S(2)}) %collective-permute-start.3) | collective-permute-done | bytes 946208 | tf_op jit(solution)/shard_map/ppermute | solution.py:23
  636.2 57.4 %pad_maximum_fusion = f32[7,22,134,512]{3,2,0,1:T(8,128)} fusion(f32[7,22,3,512]{3,2,0,1:T(4,128)} %copy.121, f32[7,3,128,512]{3,2,0,1:T(8,128)} %copy-done.6, f32[4,16,128,64]{3,2,0,1:T(8,128)S(1)} %copy-done.2, f32[4,16,128,384]{3,2,0,1:T(8,128)S(1)} %bitcast.86, f32[4,16,128,64]{3,2,0,1:T(8,128)} %copy.111, f32[7,3,128,512]{3,2,0,1:T(8,128)} %copy_select_fusion.1, ...), kind=kLoop, calls=%fused_computation | loop fusion | flops 73959424 | bytes 84525056 | tf_op jit(solution)/shard_map/concatenate | solution.py:24
  693.7 8.2 slice_bitcast_fusion.8
  701.9 25.3 %slice_bitcast_fusion.3 = (f32[22,134,512]{2,1,0:T(8,128)}, f32[22,134,512]{2,1,0:T(8,128)}, f32[22,134,512]{2,1,0:T(8,128)S(1)}, f32[22,134,512]{2,1,0:T(8,128)...) fusion(f32[7,22,134,512]{3,2,0,1:T(8,128)} %pad_maximum_fusion), kind=kLoop, calls=%fused_computation.18 | loop fusion | bytes 84525056 | tf_op jit(solution)/shard_map/squeeze | solution.py:149
  757.5 27.9 %fusion.15 = (f32[18,128,512]{2,1,0:T(8,128)}, f32[18,128,512]{2,1,0:T(8,128)}, f32[18,128,512]{2,1,0:T(8,128)}, f32[18,128,512]{2,1,0:T(8,128)}, f32[18,128,512]{2,1,0:T(8,128)}, /*index=5*/f32[18,128,512]{2,1,0:T(8,128)}) fusion(f32[22,134,512]{2,1,0:T(8,128)} %copy-done, f32[22,134,512]{2,1,0:T(8,128)} %get-tuple-element.21), kind=kLoop, calls=%fused_computation.46 | loop fusion | flops 47185920 | bytes 75497472 | tf_op jit(solution)/shard_map/sub | solution.py:50
  785.4 15.4 %subtract_negate_fusion.1 = f32[18,130,512]{2,1,0:T(8,128)} fusion(f32[22,134,512]{2,1,0:T(8,128)} %get-tuple-element.24, f32[22,134,512]{2,1,0:T(8,128)} %get-tuple-element.21, f32[22,134,512]{2,1,0:T(8,128)} %get-tuple-element.18, f32[22,134,512]{2,1,0:T(8,128)} %get-tuple-element.23), kind=kLoop, calls=%fused_computation.35 | loop fusion | flops 9584640 | bytes 33546240 | tf_op jit(solution)/shard_map/neg | solution.py:137
  800.8 23.7 %subtract_negate_fusion.2 = (f32[18,130,512]{2,1,0:T(8,128)}, f32[18,130,512]{2,1,0:T(8,128)}) fusion(f32[22,134,512]{2,1,0:T(8,128)} %copy-done.1, f32[22,134,512]{2,1,0:T(8,128)} %get-tuple-element.21, f32[22,134,512]{2,1,0:T(8,128)} %get-tuple-element.18, f32[18,130,1]{2,1,0:T(8,128)S(1)} %slice.613, f32[18,130,511]{2,1,0:T(8,128)} %slice.612, ...), kind=kLoop, calls=%fused_computation.36 | loop fusion | flops 17971200 | bytes 52715520 | tf_op jit(solution)/shard_map/neg | solution.py:138
  849.1 16.7 %minimum_add_fusion = (f32[16,128,512]{2,1,0:T(8,128)}, f32[16,128,512]{2,1,0:T(8,128)}) fusion(f32[16,128,2]{2,1,0:T(8,128)S(1)} %reshape.113, f32[16,128,510]{2,1,0:T(8,128)S(1)} %copy-done.9, f32[16,128,510]{2,1,0:T(8,128)S(1)} %copy-done.7, f32[16,128,2]{2,1,0:T(8,128)S(1)} %reshape.112, f32[22,134,512]{2,1,0:T(8,128)S(1)} %bitcast.84, ...), kind=kLoop, calls=%fused_computation.206 | loop fusion | flops 62914560 | bytes 50331648 | tf_op jit(solution)/shard_map/add | solution.py:53
  870.6 21.0 %divide_select_fusion = f32[16,128,512]{2,1,0:T(8,128)} fusion(f32[16,128,511]{2,1,0:T(8,128)} %bitcast.111, f32[16,128,1]{2,1,0:T(8,128)} %slice.578, f32[16,128,2]{2,1,0:T(8,128)S(1)} %reshape.113, f32[16,128,510]{2,1,0:T(8,128)} %get-tuple-element.46, f32[16,128,510]{2,1,0:T(8,128)S(1)} %copy-done.8, f32[16,128,2]{2,1,0:T(8,128)S(1)} %reshape.112, ...), kind=kLoop, calls=%fused_computation.205 | loop fusion | flops 83886080 | bytes 54526464 | tf_op jit(solution)/shard_map/jit(_where)/select_n | solution.py:95
  897.1 9.5 fusion.10
  906.7 11.6 %fusion.39 = (f32[16,130,512]{2,1,0:T(8,128)}, f32[16,130,512]{2,1,0:T(8,128)}, f32[16,130,512]{2,1,0:T(8,128)}, f32[16,130,512]{2,1,0:T(8,128)}, f32[16,130,512]{2,1,0:T(8,128)}, /*index=5*/f32[16,130,512]{2,1,0:T(8,128)}) fusion(f32[16,134,512]{2,1,0:T(8,128)S(1)} %bitcast.92, f32[16,134,512]{2,1,0:T(8,128)S(1)} %bitcast.90), kind=kLoop, calls=%fused_computation.82 | loop fusion | flops 42598400 | bytes 68157440 | tf_op jit(solution)/shard_map/sub | solution.py:50
  931.7 16.6 %subtract_divide_fusion = f32[16,129,512]{2,1,0:T(8,128)} fusion(f32[16,130,512]{2,1,0:T(8,128)S(1)} %bitcast.108, f32[16,130,512]{2,1,0:T(8,128)S(1)} %bitcast.110, f32[16,130,512]{2,1,0:T(8,128)S(1)} %bitcast.106, f32[16,130,512]{2,1,0:T(8,128)} %get-tuple-element.73, f32[16,130,512]{2,1,0:T(8,128)} %get-tuple-element.72, ...), kind=kLoop, calls=%fused_computation.131 | loop fusion | flops 43327488 | bytes 54951936 | tf_op jit(solution)/shard_map/div | solution.py:60
  948.2 20.9 %subtract_divide_fusion.1 = f32[17,128,512]{2,1,0:T(8,128)} fusion(f32[18,128,512]{2,1,0:T(8,128)} %get-tuple-element.51, f32[18,128,512]{2,1,0:T(8,128)} %get-tuple-element.52, f32[18,128,512]{2,1,0:T(8,128)} %get-tuple-element.50, f32[18,128,512]{2,1,0:T(8,128)} %get-tuple-element.76, f32[18,128,512]{2,1,0:T(8,128)} %get-tuple-element.75, ...), kind=kLoop, calls=%fused_computation.132 | loop fusion | flops 45678592 | bytes 57933824 | tf_op jit(solution)/shard_map/div | solution.py:60
  969.2 10.8 %fusion.83 = f32[16,128,512]{2,1,0:T(8,128)} fusion(f32[16,129,512]{2,1,0:T(8,128)} %subtract_divide_fusion, f32[17,128,512]{2,1,0:T(8,128)} %subtract_divide_fusion.1, f32[16,128,512]{2,1,0:T(8,128)S(1)} %copy-done.10, f32[16,128,511]{2,1,0:T(8,128)} %slice.580, f32[22,134,512]{2,1,0:T(8,128)S(1)} %bitcast.84), kind=kLoop, calls=%fused_computation.162 | loop fusion | flops 9437184 | bytes 33546240 | tf_op jit(solution)/shard_map/sub | solution.py:121
  980.0 24.2 %fusion.77 = (f32[1,16,128,512]{3,2,1,0:T(8,128)}, f32[1,16,128,512]{3,2,1,0:T(8,128)}, f32[1,16,128,512]{3,2,1,0:T(8,128)}) fusion(f32[17,129,512]{2,1,0:T(8,128)} %fusion.10, f32[17,128,512]{2,1,0:T(8,128)} %copy-done.4, f32[17,128,1]{2,1,0:T(8,128)S(1)} %copy-done.12, f32[17,128,511]{2,1,0:T(8,128)} %get-tuple-element.56, ...), kind=kLoop, calls=%fused_computation.153 | loop fusion | flops 25165824 | bytes 71598080 | tf_op jit(solution)/shard_map/stack | solution.py:163
  1004.2 12.1 %pad_maximum_fusion.2 = f32[3,16,128,512]{3,2,1,0:T(8,128)} fusion(f32[1,16,128,512]{3,2,1,0:T(8,128)} %get-tuple-element.54, f32[1,16,128,512]{3,2,1,0:T(8,128)} %get-tuple-element.55, f32[1,16,128,512]{3,2,1,0:T(8,128)} %get-tuple-element.53), kind=kLoop, calls=%fused_computation.14 | loop fusion | flops 6291456 | bytes 25165824 | tf_op jit(solution)/shard_map/stack | solution.py:163
  (149 shorter events, 143.9 us)
Async XLA Ops:
  11.4 96.8 %all-to-all-start = ((f32[4,16,128,128]{3,1,0,2:T(8,128)}), f32[4,16,128,128]{3,1,0,2:T(8,128)}, u32[]{:S(2)}, u32[]{:S(2)}) async-start(f32[4,16,128,128]{3,1,0,2:T(8,128)} %copy.106), calls=%async_computation | async-start | bytes 8388608 | tf_op jit(solution)/shard_map/all_to_all | solution.py:202
  285.4 97.2 %all-to-all-start.1 = ((f32[16,1,65536]{2,1,0:T(1,128)}), f32[16,1,65536]{2,1,0:T(1,128)}, u32[]{:S(2)}, u32[]{:S(2)}) async-start(f32[16,1,65536]{2,1,0:T(1,128)} %reshape.119), calls=%async_computation.1 | async-start | bytes 8388608 | tf_op jit(solution)/shard_map/all_to_all | solution.py:224
  464.0 119.5 %collective-permute-start.1 = (f32[7,3,128,512]{3,2,1,0:T(8,128)}, f32[7,3,128,512]{3,2,1,0:T(8,128)}, u32[]{:S(2)}, u32[]{:S(2)}) collective-permute-start(f32[7,3,128,512]{3,2,1,0:T(8,128)} %copy.116), channel_id=1, source_target_pairs={{16,0},{17,1},{18,2},{19,3},{20,4},{21,5},{22,6},{23,7},{24,8},{25... | collective-permute-start | bytes 16515080 | tf_op jit(solution)/shard_map/ppermute | solution.py:23
  471.9 121.2 %collective-permute-start = (f32[7,3,128,512]{3,2,1,0:T(8,128)}, f32[7,3,128,512]{3,2,1,0:T(8,128)}, u32[]{:S(2)}, u32[]{:S(2)}) collective-permute-start(f32[7,3,128,512]{3,2,1,0:T(8,128)} %copy.114), channel_id=1, source_target_pairs={{0,16},{1,17},{2,18},{3,19},{4,20},{5,21},{6,22},{7,23},{8,24},{9,... | collective-permute-start | bytes 16515080 | tf_op jit(solution)/shard_map/ppermute | solution.py:22
  583.5 16.9 %slice-start.2 = ((s8[12582912]{0:T(1024)(128)(4,1)}), s8[4194304]{0:T(1024)(128)(4,1)S(1)}, s32[]{:S(2)}) async-start(s8[12582912]{0:T(1024)(128)(4,1)} %bitcast.85), calls=%async_computation.4 | async-start | bytes 8388608
  583.5 16.9 %slice-start.3 = ((s8[12582912]{0:T(1024)(128)(4,1)}), s8[4194304]{0:T(1024)(128)(4,1)S(1)}, s32[]{:S(2)}) async-start(s8[12582912]{0:T(1024)(128)(4,1)} %bitcast.85), calls=%async_computation.5 | async-start | bytes 8388608
  587.1 13.2 %copy-start.6 = (f32[7,3,128,512]{3,2,0,1:T(8,128)}, f32[7,3,128,512]{3,2,0,1:T(8,128)S(1)}, u32[]{:S(2)}) copy-start(f32[7,3,128,512]{3,2,0,1:T(8,128)S(1)} %copy_select_fusion) | copy-start | bytes 16515076
  593.1 8.8 copy-start.3
  605.0 27.8 %collective-permute-start.3 = (f32[7,22,3,512]{3,1,2,0:T(8,128)S(1)}, f32[7,22,3,512]{3,1,2,0:T(8,128)S(1)}, u32[]{:S(2)}, u32[]{:S(2)}) collective-permute-start(f32[7,22,3,512]{3,1,2,0:T(8,128)S(1)} %copy.119), channel_id=1, source_target_pairs={{1,0},{2,1},{3,2},{4,3},{5,4},{6,5},{7,6},{8,7},{9,8},{10,9},{11,1... | collective-permute-start | bytes 2838536 | tf_op jit(solution)/shard_map/ppermute | solution.py:23
  607.5 27.1 %collective-permute-start.2 = (f32[7,22,3,512]{3,1,2,0:T(8,128)S(1)}, f32[7,22,3,512]{3,1,2,0:T(8,128)S(1)}, u32[]{:S(2)}, u32[]{:S(2)}) collective-permute-start(f32[7,22,3,512]{3,1,2,0:T(8,128)S(1)} %copy.118), channel_id=1, source_target_pairs={{0,1},{1,2},{2,3},{3,4},{4,5},{5,6},{6,7},{7,8},{8,9},{9,10},{10,1... | collective-permute-start | bytes 2838536 | tf_op jit(solution)/shard_map/ppermute | solution.py:22
  727.2 20.3 %copy-start.1 = (f32[22,134,512]{2,1,0:T(8,128)}, f32[22,134,512]{2,1,0:T(8,128)S(1)}, u32[]{:S(2)}) copy-start(f32[22,134,512]{2,1,0:T(8,128)S(1)} %get-tuple-element.20) | copy-start | bytes 18112516
  742.2 10.5 %slice-start.19 = ((s8[6127616]{0:T(1024)(128)(4,1)}), s8[4194304]{0:T(1024)(128)(4,1)S(1)}, s32[]{:S(2)}) async-start(s8[6127616]{0:T(1024)(128)(4,1)} %bitcast.103), calls=%async_computation.21 | async-start | bytes 8388608
  836.3 11.2 %slice-start = ((s8[6127616]{0:T(1024)(128)(4,1)}), s8[4194304]{0:T(1024)(128)(4,1)S(1)}, s32[]{:S(2)}) async-start(s8[6127616]{0:T(1024)(128)(4,1)} %bitcast.83), calls=%async_computation.2 | async-start | bytes 8388608
  836.3 11.2 %slice-start.5 = ((s8[6127616]{0:T(1024)(128)(4,1)}), s8[4194304]{0:T(1024)(128)(4,1)S(1)}, s32[]{:S(2)}) async-start(s8[6127616]{0:T(1024)(128)(4,1)} %bitcast.87), calls=%async_computation.7 | async-start | bytes 8388608
  836.9 10.6 %slice-start.1 = ((s8[6127616]{0:T(1024)(128)(4,1)}), s8[1933312]{0:T(1024)(128)(4,1)S(1)}, s32[]{:S(2)}) async-start(s8[6127616]{0:T(1024)(128)(4,1)} %bitcast.83), calls=%async_computation.3 | async-start | bytes 3866624
  836.9 10.6 %slice-start.6 = ((s8[6127616]{0:T(1024)(128)(4,1)}), s8[1933312]{0:T(1024)(128)(4,1)S(1)}, s32[]{:S(2)}) async-start(s8[6127616]{0:T(1024)(128)(4,1)} %bitcast.87), calls=%async_computation.8 | async-start | bytes 3866624
  849.1 21.5 %copy-start.14 = (pred[512]{0:T(512)(128)(4,1)S(1)}, pred[512]{0:T(512)(128)(4,1)}, u32[]{:S(2)}) copy-start(pred[512]{0:T(512)(128)(4,1)} %iota_compare_fusion.3) | copy-start | bytes 1540
  891.6 15.0 %slice-start.7 = ((s8[4456448]{0:T(1024)(128)(4,1)}), s8[4194304]{0:T(1024)(128)(4,1)S(1)}, s32[]{:S(2)}) async-start(s8[4456448]{0:T(1024)(128)(4,1)} %bitcast.89), calls=%async_computation.9 | async-start | bytes 8388608
  891.6 15.0 %slice-start.9 = ((s8[4456448]{0:T(1024)(128)(4,1)}), s8[4194304]{0:T(1024)(128)(4,1)S(1)}, s32[]{:S(2)}) async-start(s8[4456448]{0:T(1024)(128)(4,1)} %bitcast.91), calls=%async_computation.11 | async-start | bytes 8388608
  897.1 9.5 slice-start.8
  897.1 9.5 slice-start.10
  906.6 11.6 %slice-start.17 = ((s8[5013504]{0:T(1024)(128)(4,1)}), s8[4194304]{0:T(1024)(128)(4,1)S(1)}, s32[]{:S(2)}) async-start(s8[5013504]{0:T(1024)(128)(4,1)} %bitcast.101), calls=%async_computation.19 | async-start | bytes 8388608
  906.7 11.6 %slice-start.18 = ((s8[5013504]{0:T(1024)(128)(4,1)}), s8[819200]{0:T(1024)(128)(4,1)S(1)}, s32[]{:S(2)}) async-start(s8[5013504]{0:T(1024)(128)(4,1)} %bitcast.101), calls=%async_computation.20 | async-start | bytes 1638400
  923.7 7.9 slice-start.25
  923.7 7.9 slice-start.22
  923.7 7.9 slice-start.24
  923.7 8.0 slice-start.26
  931.7 48.3 %slice-start.11 = ((s8[6127616]{0:T(1024)(128)(4,1)}), s8[4194304]{0:T(1024)(128)(4,1)S(1)}, s32[]{:S(2)}) async-start(s8[6127616]{0:T(1024)(128)(4,1)} %bitcast.93), calls=%async_computation.13 | async-start | bytes 8388608
  948.2 20.9 %copy-start.10 = (f32[16,128,512]{2,1,0:T(8,128)S(1)}, f32[16,128,512]{2,1,0:T(8,128)}, u32[]{:S(2)}) copy-start(f32[16,128,512]{2,1,0:T(8,128)} %divide_select_fusion) | copy-start | bytes 12582916
  948.2 31.8 %slice-start.12 = ((s8[6127616]{0:T(1024)(128)(4,1)}), s8[1933312]{0:T(1024)(128)(4,1)S(1)}, s32[]{:S(2)}) async-start(s8[6127616]{0:T(1024)(128)(4,1)} %bitcast.93), calls=%async_computation.14 | async-start | bytes 3866624
  969.2 10.8 %copy-start.12 = (f32[17,128,1]{2,1,0:T(8,128)S(1)}, f32[17,128,1]{2,1,0:T(8,128)}, u32[]{:S(2)}) copy-start(f32[17,128,1]{2,1,0:T(8,128)} %get-tuple-element.58) | copy-start | bytes 26116
  969.2 10.8 %copy-start.13 = (f32[16,129,1]{2,1,0:T(8,128)S(1)}, f32[16,129,1]{2,1,0:T(8,128)}, u32[]{:S(2)}) copy-start(f32[16,129,1]{2,1,0:T(8,128)} %get-tuple-element.61) | copy-start | bytes 24772
  (16 other events, 89.2 us)
where the time goes:
time: 1020 us
  other arithmetic  409 us (40%)
  waiting for transfers between devices  232 us (23%)
  local copies, waits for them, and re-layouts  220 us (22%)
  matrix products  128 us (13%)
  starting transfers between devices  25 us (2%)
    ppermute x2, waiting for transfers between devices, extended(): after = lax.ppermute(leading, axis, down)  128 us
    dot_general x1, matrix products, per_device(): lax.dot_general(spectrum.reshape(-1, NP), fourier_basis, (((1,), (1,)), (...  94.4 us
    all_to_all x1, waiting for transfers between devices, per_device(): lax.all_to_all(smoothed, 'phi', split_axis=3, concat_axis=2, tiled=True)  78.6 us
    dot_general x1, other arithmetic, per_device(): jnp.dot(lines.reshape(-1, NP), fourier_basis, precision=lax.Precision.HIG...  67.5 us
    concatenate x1, other arithmetic, extended(): value = jnp.concatenate([before, value, after], axis=dim)  57.4 us
    unnamed x86, local copies, waits for them, and re-layouts  55.7 us
    sub x2, other arithmetic, edge_values(): to_right = right_face - centre  39.5 us
    div x2, other arithmetic, hll_flux(): (upwind + slowest * fastest * (dens_right - dens_left)) / (fastest - slow...  37.5 us
  transfers between devices with their start and end apart: 6, of which 5 were waited for; matrix products, arithmetic and copies ran while one was open for 9% of the time, Pallas kernels for 0%

commit v1 on v0

--- a/solution.py
+++ b/solution.py
@@ -221,7 +221,9 @@
         precision=lax.Precision.HIGHEST,
         preferred_element_type=jnp.float32,
     ).reshape(lines.shape)
-    returned = lax.all_to_all(smoothed, "phi", split_axis=3, concat_axis=2, tiled=True)
+    pieces = jnp.split(smoothed, lax.axis_size("phi"), axis=3)
+    received = lax.all_to_all(jnp.stack(pieces), "phi", 0, 0)
+    returned = jnp.concatenate(received, axis=2)
     returned = jnp.swapaxes(returned, 2, 3)
     primitive = jnp.concatenate(
         [

time: 1020 us -> 924 us (0.906)
  local copies, waits for them, and re-layouts: 220 us -> 137 us
  other arithmetic: 409 us -> 396 us
    unnamed x86 -> x99, local copies, waits for them, and re-layouts: 55.7 us -> 19 us
    dot_general x1 -> x0, local copies, waits for them, and re-layouts: 26.4 us -> none  [per_device(): lax.dot_general(spectrum.reshape(-1, NP), fourier_basis, (((1,), (1,)), (...]
    all_to_all x2 -> x0, local copies, waits for them, and re-layouts: 21.6 us -> none  [per_device(): lax.all_to_all(smoothed, 'phi', split_axis=3, concat_axis=2, tiled=True)]
    all_to_all x1 -> x0, other arithmetic: 13.7 us -> none  [per_device(): lax.all_to_all(smoothed, 'phi', split_axis=3, concat_axis=2, tiled=True)]
  transfers between devices with their start and end apart: 6 -> 6, of which waited for: 5 -> 5; matrix products, arithmetic and copies ran while one was open for 9% -> 10% of each run, Pallas kernels for 0% -> 0%
where the time goes in v1:
time: 924 us; the launch traced here: 919 us
  other arithmetic  396 us (43%)
  waiting for transfers between devices  232 us (25%)
  local copies, waits for them, and re-layouts  137 us (15%)
  matrix products  128 us (14%)
  starting transfers between devices  25.1 us (3%)
    ppermute x2, waiting for transfers between devices, extended(): after = lax.ppermute(leading, axis, down)  128 us
    dot_general x1, matrix products, per_device(): lax.dot_general(spectrum.reshape(-1, NP), fourier_basis, (((1,), (1,)), (...  93.7 us
    all_to_all x1, waiting for transfers between devices, per_device(): received = lax.all_to_all(jnp.stack(pieces), 'phi', 0, 0)  78.6 us
    dot_general x1, other arithmetic, per_device(): jnp.dot(lines.reshape(-1, NP), fourier_basis, precision=lax.Precision.HIG...  67.5 us
    concatenate x1, other arithmetic, extended(): value = jnp.concatenate([before, value, after], axis=dim)  57.5 us
    sub x2, other arithmetic, edge_values(): to_right = right_face - centre  39.5 us
    div x2, other arithmetic, hll_flux(): (upwind + slowest * fastest * (dens_right - dens_left)) / (fastest - slow...  37.3 us
    another operation x2, other arithmetic, advance(): return (density_next, jnp.stack([radial_next, polar_next, azimuth_next]))  36.3 us
  transfers between devices with their start and end apart: 6, of which 5 were waited for; matrix products, arithmetic and copies ran while one was open for 10% of the time, Pallas kernels for 0%

profile of v1, /device:TPU:13, one launch (start us, length us, event | category | flops | bytes accessed | tf_op | source)
XLA Modules:
  0.0 918.6 jit_solution(13087565515550808105)
XLA Ops:
  6.0 5.4 copy.86
  11.4 6.5 all-to-all-start
  20.5 67.5 %fusion.169 = f32[2048,2048,1,1]{1,0,3,2:T(8,128)} fusion(s32[2048]{0:T(1024)S(1)} %iota_add_fusion, pred[2048]{0:T(1024)(128)(4,1)S(1)} %iota_compare_fusion.2), kind=kLoop, calls=%fused_computation.10.clone.1 | loop fusion | flops 67108864 | bytes 16787456 | tf_op jit(solution)/shard_map/dot_general | solution.py:210
  88.0 20.2 %all-to-all-done = f32[4,16,128,128]{3,1,0,2:T(8,128)} async-done(((f32[4,16,128,128]{3,1,0,2:T(8,128)}), f32[4,16,128,128]{3,1,0,2:T(8,128)}, u32[]{:S(2)}, u32[]{:S(2)}) %all-to-all-start) | async-done | bytes 4194336 | tf_op jit(solution)/shard_map/all_to_all | solution.py:202
  108.2 33.9 %fusion.5 = f32[4,16,8,2048]{3,2,1,0:T(8,128)S(1)} fusion(f32[4,16,128,128]{3,1,0,2:T(8,128)} %all-to-all-done, f32[2048,2048,1,1]{1,0,3,2:T(8,128)} %fusion.169), kind=kOutput, calls=%fused_computation.9 | convolution fusion | flops 25769803776 | bytes 25165824 | tf_op jit(solution)/shard_map/dot_general | solution.py:210
  142.4 93.7 %fusion.3 = f32[4,16,8,2048]{3,2,1,0:T(8,128)S(1)} fusion(pred[2048]{0:T(1024)(128)(4,1)S(1)} %iota_compare_fusion.2, s32[2048]{0:T(1024)S(1)} %iota_add_fusion, f32[4,16,8,2048]{3,2,1,0:T(8,128)S(1)} %fusion.167), kind=kOutput, calls=%fused_computation.7 | convolution fusion | flops 25836912640 | bytes 8398848 | tf_op jit(solution)/shard_map/dot_general | solution.py:217
  247.9 7.0 all-to-all-start.1
  255.0 11.6 %pad_maximum_fusion.1 = f32[4,16,128,384]{3,2,0,1:T(8,128)} fusion(f32[1,16,128,512]{3,2,0,1:T(8,128)} %bitcast.174, f32[3,16,128,512]{3,2,1,0:T(8,128)} %param.4), kind=kLoop, calls=%fused_computation.13 | loop fusion | flops 3145728 | bytes 29360128 | tf_op jit(solution)/shard_map/concatenate | solution.py:185
  266.6 78.6 %all-to-all-done.1 = f32[16,4,16,8,128]{4,3,2,1,0:T(8,128)} async-done(((f32[16,4,16,8,128]{4,3,2,1,0:T(8,128)}), f32[16,4,16,8,128]{4,3,2,1,0:T(8,128)}, u32[]{:S(2)}, u32[]{:S(2)}) %all-to-all-start.1) | async-done | bytes 4194336 | tf_op jit(solution)/shard_map/all_to_all | solution.py:225
  356.3 6.3 pad_maximum_fusion.6
  379.2 106.2 %collective-permute-done.1 = f32[7,3,128,512]{3,2,1,0:T(8,128)} collective-permute-done((f32[7,3,128,512]{3,2,1,0:T(8,128)}, f32[7,3,128,512]{3,2,1,0:T(8,128)}, u32[]{:S(2)}, u32[]{:S(2)}) %collective-permute-start.1) | collective-permute-done | bytes 5505056 | tf_op jit(solution)/shard_map/ppermute | solution.py:23
  489.0 5.8 collective-permute-done
  494.8 7.3 copy_select_fusion.1
  513.4 21.5 %collective-permute-done.3 = f32[7,22,3,512]{3,1,2,0:T(8,128)S(1)} collective-permute-done((f32[7,22,3,512]{3,1,2,0:T(8,128)S(1)}, f32[7,22,3,512]{3,1,2,0:T(8,128)S(1)}, u32[]{:S(2)}, u32[]{:S(2)}) %collective-permute-start.3) | collective-permute-done | bytes 946208 | tf_op jit(solution)/shard_map/ppermute | solution.py:23
  538.2 57.5 %pad_maximum_fusion = f32[7,22,134,512]{3,2,0,1:T(8,128)} fusion(f32[7,22,3,512]{3,2,0,1:T(4,128)} %copy.99, f32[7,3,128,512]{3,2,0,1:T(8,128)} %copy-done.6, f32[4,16,128,64]{3,2,0,1:T(8,128)S(1)} %copy-done.2, f32[4,16,128,384]{3,2,0,1:T(8,128)S(1)} %bitcast.148, f32[4,16,128,64]{3,2,0,1:T(8,128)} %copy.89, f32[7,3,128,512]{3,2,0,1:T(8,128)} %copy_select_fusion.1, ...), kind=kLoop, calls=%fused_computation | loop fusion | flops 73959424 | bytes 84525056 | tf_op jit(solution)/shard_map/concatenate | solution.py:24
  595.7 8.2 slice_bitcast_fusion.8
  603.9 25.5 %slice_bitcast_fusion.3 = (f32[22,134,512]{2,1,0:T(8,128)}, f32[22,134,512]{2,1,0:T(8,128)}, f32[22,134,512]{2,1,0:T(8,128)S(1)}, f32[22,134,512]{2,1,0:T(8,128)...) fusion(f32[7,22,134,512]{3,2,0,1:T(8,128)} %pad_maximum_fusion), kind=kLoop, calls=%fused_computation.18 | loop fusion | bytes 84525056 | tf_op jit(solution)/shard_map/squeeze | solution.py:149
  659.6 27.9 %fusion.15 = (f32[18,128,512]{2,1,0:T(8,128)}, f32[18,128,512]{2,1,0:T(8,128)}, f32[18,128,512]{2,1,0:T(8,128)}, f32[18,128,512]{2,1,0:T(8,128)}, f32[18,128,512]{2,1,0:T(8,128)}, /*index=5*/f32[18,128,512]{2,1,0:T(8,128)}) fusion(f32[22,134,512]{2,1,0:T(8,128)} %copy-done, f32[22,134,512]{2,1,0:T(8,128)} %get-tuple-element.19), kind=kLoop, calls=%fused_computation.46 | loop fusion | flops 47185920 | bytes 75497472 | tf_op jit(solution)/shard_map/sub | solution.py:50
  687.5 15.3 %subtract_negate_fusion.1 = f32[18,130,512]{2,1,0:T(8,128)} fusion(f32[22,134,512]{2,1,0:T(8,128)} %get-tuple-element.22, f32[22,134,512]{2,1,0:T(8,128)} %get-tuple-element.19, f32[22,134,512]{2,1,0:T(8,128)} %get-tuple-element.16, f32[22,134,512]{2,1,0:T(8,128)} %get-tuple-element.21), kind=kLoop, calls=%fused_computation.35 | loop fusion | flops 9584640 | bytes 33546240 | tf_op jit(solution)/shard_map/neg | solution.py:137
  702.8 23.6 %subtract_negate_fusion.2 = (f32[18,130,512]{2,1,0:T(8,128)}, f32[18,130,512]{2,1,0:T(8,128)}) fusion(f32[22,134,512]{2,1,0:T(8,128)} %copy-done.1, f32[22,134,512]{2,1,0:T(8,128)} %get-tuple-element.19, f32[22,134,512]{2,1,0:T(8,128)} %get-tuple-element.16, f32[18,130,1]{2,1,0:T(8,128)S(1)} %slice.613, f32[18,130,511]{2,1,0:T(8,128)} %slice.612, ...), kind=kLoop, calls=%fused_computation.36 | loop fusion | flops 17971200 | bytes 52715520 | tf_op jit(solution)/shard_map/neg | solution.py:138
  738.9 5.8 fusion.149
  751.1 16.7 %minimum_add_fusion = (f32[16,128,512]{2,1,0:T(8,128)}, f32[16,128,512]{2,1,0:T(8,128)}) fusion(f32[16,128,2]{2,1,0:T(8,128)S(1)} %reshape.121, f32[16,128,510]{2,1,0:T(8,128)S(1)} %copy-done.9, f32[16,128,510]{2,1,0:T(8,128)S(1)} %copy-done.7, f32[16,128,2]{2,1,0:T(8,128)S(1)} %reshape.120, f32[22,134,512]{2,1,0:T(8,128)S(1)} %bitcast.146, ...), kind=kLoop, calls=%fused_computation.207 | loop fusion | flops 62914560 | bytes 50331648 | tf_op jit(solution)/shard_map/add | solution.py:53
  772.6 21.2 %divide_select_fusion = f32[16,128,512]{2,1,0:T(8,128)} fusion(f32[16,128,511]{2,1,0:T(8,128)} %bitcast.171, f32[16,128,1]{2,1,0:T(8,128)} %slice.578, f32[16,128,2]{2,1,0:T(8,128)S(1)} %reshape.121, f32[16,128,510]{2,1,0:T(8,128)} %get-tuple-element.44, f32[16,128,510]{2,1,0:T(8,128)S(1)} %copy-done.8, f32[16,128,2]{2,1,0:T(8,128)S(1)} %reshape.120, ...), kind=kLoop, calls=%fused_computation.206 | loop fusion | flops 83886080 | bytes 54526464 | tf_op jit(solution)/shard_map/jit(_where)/select_n | solution.py:95
  793.9 5.5 slice.580
  799.3 9.5 %fusion.10 = f32[17,129,512]{2,1,0:T(8,128)} fusion(f32[18,130,512]{2,1,0:T(8,128)} %subtract_negate_fusion.1), kind=kLoop, calls=%fused_computation.38 | loop fusion | flops 4491264 | bytes 22456320 | tf_op jit(solution)/shard_map/mul | solution.py:145
  808.9 11.6 %fusion.39 = (f32[16,130,512]{2,1,0:T(8,128)}, f32[16,130,512]{2,1,0:T(8,128)}, f32[16,130,512]{2,1,0:T(8,128)}, f32[16,130,512]{2,1,0:T(8,128)}, f32[16,130,512]{2,1,0:T(8,128)}, /*index=5*/f32[16,130,512]{2,1,0:T(8,128)}) fusion(f32[16,134,512]{2,1,0:T(8,128)S(1)} %bitcast.154, f32[16,134,512]{2,1,0:T(8,128)S(1)} %bitcast.152), kind=kLoop, calls=%fused_computation.82 | loop fusion | flops 42598400 | bytes 68157440 | tf_op jit(solution)/shard_map/sub | solution.py:50
  820.5 5.4 fusion.61
  834.0 16.5 %subtract_divide_fusion = f32[16,129,512]{2,1,0:T(8,128)} fusion(f32[16,130,512]{2,1,0:T(8,128)S(1)} %bitcast.168, f32[16,130,512]{2,1,0:T(8,128)S(1)} %bitcast.170, f32[16,130,512]{2,1,0:T(8,128)S(1)} %bitcast.166, f32[16,130,512]{2,1,0:T(8,128)} %get-tuple-element.71, f32[16,130,512]{2,1,0:T(8,128)} %get-tuple-element.70, ...), kind=kLoop, calls=%fused_computation.131 | loop fusion | flops 43327488 | bytes 54951936 | tf_op jit(solution)/shard_map/div | solution.py:60
  850.5 20.8 %subtract_divide_fusion.1 = f32[17,128,512]{2,1,0:T(8,128)} fusion(f32[18,128,512]{2,1,0:T(8,128)} %get-tuple-element.49, f32[18,128,512]{2,1,0:T(8,128)} %get-tuple-element.50, f32[18,128,512]{2,1,0:T(8,128)} %get-tuple-element.48, f32[18,128,512]{2,1,0:T(8,128)} %get-tuple-element.74, f32[18,128,512]{2,1,0:T(8,128)} %get-tuple-element.73, ...), kind=kLoop, calls=%fused_computation.132 | loop fusion | flops 45678592 | bytes 57933824 | tf_op jit(solution)/shard_map/div | solution.py:60
  871.3 10.8 %fusion.83 = f32[16,128,512]{2,1,0:T(8,128)} fusion(f32[16,129,512]{2,1,0:T(8,128)} %subtract_divide_fusion, f32[17,128,512]{2,1,0:T(8,128)} %subtract_divide_fusion.1, f32[16,128,512]{2,1,0:T(8,128)S(1)} %copy-done.10, f32[16,128,511]{2,1,0:T(8,128)} %slice.580, f32[22,134,512]{2,1,0:T(8,128)S(1)} %bitcast.146), kind=kLoop, calls=%fused_computation.162 | loop fusion | flops 9437184 | bytes 33546240 | tf_op jit(solution)/shard_map/sub | solution.py:121
  882.2 24.2 %fusion.77 = (f32[1,16,128,512]{3,2,1,0:T(8,128)}, f32[1,16,128,512]{3,2,1,0:T(8,128)}, f32[1,16,128,512]{3,2,1,0:T(8,128)}) fusion(f32[17,129,512]{2,1,0:T(8,128)} %fusion.10, f32[17,128,512]{2,1,0:T(8,128)} %copy-done.4, f32[17,128,1]{2,1,0:T(8,128)S(1)} %copy-done.12, f32[17,128,511]{2,1,0:T(8,128)} %get-tuple-element.54, ...), kind=kLoop, calls=%fused_computation.153 | loop fusion | flops 25165824 | bytes 71598080 | tf_op jit(solution)/shard_map/stack | solution.py:163
  906.3 12.1 %pad_maximum_fusion.2 = f32[3,16,128,512]{3,2,1,0:T(8,128)} fusion(f32[1,16,128,512]{3,2,1,0:T(8,128)} %get-tuple-element.52, f32[1,16,128,512]{3,2,1,0:T(8,128)} %get-tuple-element.53, f32[1,16,128,512]{3,2,1,0:T(8,128)} %get-tuple-element.51), kind=kLoop, calls=%fused_computation.14 | loop fusion | flops 6291456 | bytes 25165824 | tf_op jit(solution)/shard_map/stack | solution.py:163
  (160 shorter events, 127.6 us)
Async XLA Ops:
  11.4 96.8 %all-to-all-start = ((f32[4,16,128,128]{3,1,0,2:T(8,128)}), f32[4,16,128,128]{3,1,0,2:T(8,128)}, u32[]{:S(2)}, u32[]{:S(2)}) async-start(f32[4,16,128,128]{3,1,0,2:T(8,128)} %copy.86), calls=%async_computation | async-start | bytes 8388608 | tf_op jit(solution)/shard_map/all_to_all | solution.py:202
  247.9 97.2 %all-to-all-start.1 = ((f32[16,4,16,8,128]{4,3,2,1,0:T(8,128)}), f32[16,4,16,8,128]{4,3,2,1,0:T(8,128)}, u32[]{:S(2)}, u32[]{:S(2)}) async-start(f32[16,4,16,8,128]{4,3,2,1,0:T(8,128)} %fusion.113), calls=%async_computation.1 | async-start | bytes 8388608 | tf_op jit(solution)/shard_map/all_to_all | solution.py:225
  365.9 119.5 %collective-permute-start.1 = (f32[7,3,128,512]{3,2,1,0:T(8,128)}, f32[7,3,128,512]{3,2,1,0:T(8,128)}, u32[]{:S(2)}, u32[]{:S(2)}) collective-permute-start(f32[7,3,128,512]{3,2,1,0:T(8,128)} %copy.94), channel_id=1, source_target_pairs={{16,0},{17,1},{18,2},{19,3},{20,4},{21,5},{22,6},{23,7},{24,8},{25... | collective-permute-start | bytes 16515080 | tf_op jit(solution)/shard_map/ppermute | solution.py:23
  373.6 121.2 %collective-permute-start = (f32[7,3,128,512]{3,2,1,0:T(8,128)}, f32[7,3,128,512]{3,2,1,0:T(8,128)}, u32[]{:S(2)}, u32[]{:S(2)}) collective-permute-start(f32[7,3,128,512]{3,2,1,0:T(8,128)} %copy.92), channel_id=1, source_target_pairs={{0,16},{1,17},{2,18},{3,19},{4,20},{5,21},{6,22},{7,23},{8,24},{9,... | collective-permute-start | bytes 16515080 | tf_op jit(solution)/shard_map/ppermute | solution.py:22
  485.4 16.7 %slice-start.2 = ((s8[12582912]{0:T(1024)(128)(4,1)}), s8[4194304]{0:T(1024)(128)(4,1)S(1)}, s32[]{:S(2)}) async-start(s8[12582912]{0:T(1024)(128)(4,1)} %bitcast.147), calls=%async_computation.4 | async-start | bytes 8388608
  485.4 16.7 %slice-start.3 = ((s8[12582912]{0:T(1024)(128)(4,1)}), s8[4194304]{0:T(1024)(128)(4,1)S(1)}, s32[]{:S(2)}) async-start(s8[12582912]{0:T(1024)(128)(4,1)} %bitcast.147), calls=%async_computation.5 | async-start | bytes 8388608
  489.0 13.1 %copy-start.6 = (f32[7,3,128,512]{3,2,0,1:T(8,128)}, f32[7,3,128,512]{3,2,0,1:T(8,128)S(1)}, u32[]{:S(2)}) copy-start(f32[7,3,128,512]{3,2,0,1:T(8,128)S(1)} %copy_select_fusion) | copy-start | bytes 16515076
  494.8 8.8 copy-start.3
  506.8 28.1 %collective-permute-start.3 = (f32[7,22,3,512]{3,1,2,0:T(8,128)S(1)}, f32[7,22,3,512]{3,1,2,0:T(8,128)S(1)}, u32[]{:S(2)}, u32[]{:S(2)}) collective-permute-start(f32[7,22,3,512]{3,1,2,0:T(8,128)S(1)} %copy.97), channel_id=1, source_target_pairs={{1,0},{2,1},{3,2},{4,3},{5,4},{6,5},{7,6},{8,7},{9,8},{10,9},{11,1... | collective-permute-start | bytes 2838536 | tf_op jit(solution)/shard_map/ppermute | solution.py:23
  509.2 27.3 %collective-permute-start.2 = (f32[7,22,3,512]{3,1,2,0:T(8,128)S(1)}, f32[7,22,3,512]{3,1,2,0:T(8,128)S(1)}, u32[]{:S(2)}, u32[]{:S(2)}) collective-permute-start(f32[7,22,3,512]{3,1,2,0:T(8,128)S(1)} %copy.96), channel_id=1, source_target_pairs={{0,1},{1,2},{2,3},{3,4},{4,5},{5,6},{6,7},{7,8},{8,9},{9,10},{10,1... | collective-permute-start | bytes 2838536 | tf_op jit(solution)/shard_map/ppermute | solution.py:22
  629.4 20.3 %copy-start.1 = (f32[22,134,512]{2,1,0:T(8,128)}, f32[22,134,512]{2,1,0:T(8,128)S(1)}, u32[]{:S(2)}) copy-start(f32[22,134,512]{2,1,0:T(8,128)S(1)} %get-tuple-element.18) | copy-start | bytes 18112516
  644.4 10.6 %slice-start.19 = ((s8[6127616]{0:T(1024)(128)(4,1)}), s8[4194304]{0:T(1024)(128)(4,1)S(1)}, s32[]{:S(2)}) async-start(s8[6127616]{0:T(1024)(128)(4,1)} %bitcast.163), calls=%async_computation.21 | async-start | bytes 8388608
  738.3 11.2 %slice-start = ((s8[6127616]{0:T(1024)(128)(4,1)}), s8[4194304]{0:T(1024)(128)(4,1)S(1)}, s32[]{:S(2)}) async-start(s8[6127616]{0:T(1024)(128)(4,1)} %bitcast.145), calls=%async_computation.2 | async-start | bytes 8388608
  738.3 11.2 %slice-start.5 = ((s8[6127616]{0:T(1024)(128)(4,1)}), s8[4194304]{0:T(1024)(128)(4,1)S(1)}, s32[]{:S(2)}) async-start(s8[6127616]{0:T(1024)(128)(4,1)} %bitcast.149), calls=%async_computation.7 | async-start | bytes 8388608
  738.9 10.5 %slice-start.1 = ((s8[6127616]{0:T(1024)(128)(4,1)}), s8[1933312]{0:T(1024)(128)(4,1)S(1)}, s32[]{:S(2)}) async-start(s8[6127616]{0:T(1024)(128)(4,1)} %bitcast.145), calls=%async_computation.3 | async-start | bytes 3866624
  738.9 10.5 %slice-start.6 = ((s8[6127616]{0:T(1024)(128)(4,1)}), s8[1933312]{0:T(1024)(128)(4,1)S(1)}, s32[]{:S(2)}) async-start(s8[6127616]{0:T(1024)(128)(4,1)} %bitcast.149), calls=%async_computation.8 | async-start | bytes 3866624
  751.1 21.5 %copy-start.14 = (pred[512]{0:T(512)(128)(4,1)S(1)}, pred[512]{0:T(512)(128)(4,1)}, u32[]{:S(2)}) copy-start(pred[512]{0:T(512)(128)(4,1)} %iota_compare_fusion.3) | copy-start | bytes 1540
  793.8 15.0 %slice-start.7 = ((s8[4456448]{0:T(1024)(128)(4,1)}), s8[4194304]{0:T(1024)(128)(4,1)S(1)}, s32[]{:S(2)}) async-start(s8[4456448]{0:T(1024)(128)(4,1)} %bitcast.151), calls=%async_computation.9 | async-start | bytes 8388608
  793.8 15.0 %slice-start.9 = ((s8[4456448]{0:T(1024)(128)(4,1)}), s8[4194304]{0:T(1024)(128)(4,1)S(1)}, s32[]{:S(2)}) async-start(s8[4456448]{0:T(1024)(128)(4,1)} %bitcast.153), calls=%async_computation.11 | async-start | bytes 8388608
  799.3 9.5 %slice-start.8 = ((s8[4456448]{0:T(1024)(128)(4,1)}), s8[262144]{0:T(1024)(128)(4,1)S(1)}, s32[]{:S(2)}) async-start(s8[4456448]{0:T(1024)(128)(4,1)} %bitcast.151), calls=%async_computation.10 | async-start | bytes 524288
  799.3 9.5 %slice-start.10 = ((s8[4456448]{0:T(1024)(128)(4,1)}), s8[262144]{0:T(1024)(128)(4,1)S(1)}, s32[]{:S(2)}) async-start(s8[4456448]{0:T(1024)(128)(4,1)} %bitcast.153), calls=%async_computation.12 | async-start | bytes 524288
  808.8 11.7 %slice-start.17 = ((s8[5013504]{0:T(1024)(128)(4,1)}), s8[4194304]{0:T(1024)(128)(4,1)S(1)}, s32[]{:S(2)}) async-start(s8[5013504]{0:T(1024)(128)(4,1)} %bitcast.161), calls=%async_computation.19 | async-start | bytes 8388608
  808.9 11.6 %slice-start.18 = ((s8[5013504]{0:T(1024)(128)(4,1)}), s8[819200]{0:T(1024)(128)(4,1)S(1)}, s32[]{:S(2)}) async-start(s8[5013504]{0:T(1024)(128)(4,1)} %bitcast.161), calls=%async_computation.20 | async-start | bytes 1638400
  826.0 7.9 slice-start.25
  826.0 7.9 slice-start.22
  826.0 7.9 slice-start.24
  826.0 8.0 slice-start.26
  834.0 48.1 %slice-start.11 = ((s8[6127616]{0:T(1024)(128)(4,1)}), s8[4194304]{0:T(1024)(128)(4,1)S(1)}, s32[]{:S(2)}) async-start(s8[6127616]{0:T(1024)(128)(4,1)} %bitcast.155), calls=%async_computation.13 | async-start | bytes 8388608
  850.5 20.8 %copy-start.10 = (f32[16,128,512]{2,1,0:T(8,128)S(1)}, f32[16,128,512]{2,1,0:T(8,128)}, u32[]{:S(2)}) copy-start(f32[16,128,512]{2,1,0:T(8,128)} %divide_select_fusion) | copy-start | bytes 12582916
  850.5 31.7 %slice-start.12 = ((s8[6127616]{0:T(1024)(128)(4,1)}), s8[1933312]{0:T(1024)(128)(4,1)S(1)}, s32[]{:S(2)}) async-start(s8[6127616]{0:T(1024)(128)(4,1)} %bitcast.155), calls=%async_computation.14 | async-start | bytes 3866624
  871.3 10.9 %copy-start.12 = (f32[17,128,1]{2,1,0:T(8,128)S(1)}, f32[17,128,1]{2,1,0:T(8,128)}, u32[]{:S(2)}) copy-start(f32[17,128,1]{2,1,0:T(8,128)} %get-tuple-element.56) | copy-start | bytes 26116
  871.3 10.9 %copy-start.13 = (f32[16,129,1]{2,1,0:T(8,128)S(1)}, f32[16,129,1]{2,1,0:T(8,128)}, u32[]{:S(2)}) copy-start(f32[16,129,1]{2,1,0:T(8,128)} %get-tuple-element.59) | copy-start | bytes 24772
  (16 other events, 89.3 us)
